TPU v7x, 256 devices: a whole 4x4x8 slice. The times are simulated.
256 devices in a mesh: section: 8 (over z_lo, y), dp: 32 (over x, z_hi, core).
Axes of the slice: x: 4, y: 4, z: 8 (z_hi: 4, z_lo: 2; z = z_hi * 2 + z_lo), core: 2. Of those that a mesh axis runs over, the one named last changes fastest.
Arguments:
- inputs: bfloat16 [256, 128, 1536], P('dp'), parts along dimension 0, may hold values from -6 to 6
- w_query: bfloat16 [8, 1536, 768], P('section'), may hold values from -0.15625 to 0.15625
- w_key: bfloat16 [8, 1536, 768], P('section'), may hold values from -0.15625 to 0.15625
- w_value: bfloat16 [8, 1536, 768], P('section'), may hold values from -0.15625 to 0.15625
- w_out: bfloat16 [8, 768, 1536], P('section'), may hold values from -0.21875 to 0.21875
- mixing: float32 [8], P('section'), may hold values from 0.2 to 0.8
Outputs:
- outputs: bfloat16 [256, 128, 1536], P(('dp', 'section')), parts along dimension 0
There are 32 independent parts, one for each index of `dp`. A program takes and returns all parts, laid end to end along the dimension named above; an argument that names none is the same for every part. Nothing has to cross between parts.
All inputs are finite; a program needn't handle non-finite values.
Results may differ from a plain program's by a relative error of at most 0.023.
Values may be sent and summed in bfloat16 or wider, within the bound.
A program may use at most 128 MiB of HBM per device.

v0:
```python
import jax
import jax.numpy as jnp
from jax import lax
from jax.sharding import PartitionSpec as P

HEADS = 6


epsilon = 1e-06
score_scale = 0.12


def shifted(value, axis, steps):
    count = lax.axis_size(axis)
    first, last = (max(0, -steps), min(count, count - steps))
    return lax.ppermute(value, axis, [(source, source + steps) for source in range(first, last)])


def norm_rows(tensor):
    return tensor * lax.rsqrt(jnp.mean(tensor * tensor, axis=-1, keepdims=True) + epsilon)


def project(normed, weight):
    return jnp.dot(normed, weight, preferred_element_type=jnp.float32)


def layer_apply(hidden, w_query, w_key, w_value, w_out, mixing, first_values, first_flag):
    row_count = hidden.shape[0]
    hidden_wide = hidden.astype(jnp.float32)
    normed = norm_rows(hidden_wide).astype(jnp.bfloat16)
    queries = norm_rows(project(normed, w_query).reshape(row_count, HEADS, -1)).astype(jnp.bfloat16)
    key_rows = norm_rows(project(normed, w_key).reshape(row_count, HEADS, -1)).astype(jnp.bfloat16)
    values = project(normed, w_value)
    own_values = values.astype(jnp.bfloat16)
    blended = (mixing * values + (1.0 - mixing) * first_values.astype(jnp.float32)).astype(
        jnp.bfloat16
    )
    used_values = jnp.where(first_flag, own_values, blended).reshape(row_count, HEADS, -1)
    scores = (
        jnp.einsum("qhd,khd->hqk", queries, key_rows, preferred_element_type=jnp.float32)
        * score_scale
    )
    positions = jnp.arange(row_count, dtype=jnp.int32)
    causal = positions[:, None] >= positions[None, :]
    weights = jnp.where(causal[None, :, :], jnp.exp(scores), 0.0)
    probabilities = (weights / jnp.sum(weights, axis=-1, keepdims=True)).astype(jnp.bfloat16)
    attended = jnp.einsum(
        "hqk,khd->qhd", probabilities, used_values, preferred_element_type=jnp.float32
    )
    attended = attended.astype(jnp.bfloat16).reshape(row_count, -1)
    result = (hidden_wide + project(attended, w_out)).astype(jnp.bfloat16)
    return (result, own_values)


def body(inputs, w_query, w_key, w_value, w_out, mixing):
    section_count = lax.axis_size("section")
    section_index = lax.axis_index("section")
    micro_count, row_count, model_width = inputs.shape
    value_width = w_value.shape[2]
    step_count = micro_count + section_count - 1
    last_section = section_count - 1
    share_count = micro_count // section_count

    def run_layers(hidden, first_values):
        current = first_values
        first_flag = jnp.logical_and(section_index == 0, 0 == 0)
        hidden, own_values = layer_apply(
            hidden, w_query[0], w_key[0], w_value[0], w_out[0], mixing[0], current, first_flag
        )
        current = jnp.where(section_index == 0, own_values, current)
        return (hidden, current)

    def advance(time_step, carried):
        received, value_store, outputs = carried
        micro_index = time_step - section_index
        active = jnp.logical_and(micro_index >= 0, micro_index < micro_count)
        slot_index = jnp.clip(micro_index, 0, micro_count - 1)
        fresh_rows = lax.dynamic_index_in_dim(
            inputs, jnp.minimum(time_step, micro_count - 1), 0, keepdims=False
        )
        hidden = jnp.where(section_index == 0, fresh_rows, received)
        first_values = value_store

        def run_section(operands):
            section_rows, section_first = operands
            return run_layers(section_rows, section_first)

        def pass_through(operands):
            return operands

        result, current = lax.cond(active, run_section, pass_through, (hidden, first_values))
        previous = lax.dynamic_index_in_dim(outputs, slot_index, 0, keepdims=False)
        finished = jnp.where(
            jnp.logical_and(active, section_index == last_section), result, previous
        )
        outputs = lax.dynamic_update_index_in_dim(outputs, finished, slot_index, 0)
        received, value_store = shifted((result, current), "section", 1)
        return (received, value_store, outputs)

    value_store = jnp.zeros((row_count, value_width), jnp.bfloat16)
    received = jnp.zeros((row_count, model_width), jnp.bfloat16)
    outputs = jnp.zeros((micro_count, row_count, model_width), jnp.bfloat16)
    received, value_store, outputs = lax.fori_loop(
        0, step_count, advance, (received, value_store, outputs)
    )
    gathered = lax.all_to_all(outputs, "section", split_axis=0, concat_axis=0, tiled=True)
    return gathered[last_section * share_count :]


def solution(mesh):
    in_specs = (
        P("dp", None, None),
        P("section", None, None),
        P("section", None, None),
        P("section", None, None),
        P("section", None, None),
        P("section"),
    )
    out_specs = P(("dp", "section"), None, None)
    return jax.shard_map(body, mesh=mesh, in_specs=in_specs, out_specs=out_specs, check_vma=False)
```

profile of v0, /device:TPU:184, one launch (start us, length us, event | category | flops | bytes accessed | tf_op | source)
XLA Modules:
  0.0 446.2 jit_solution(13528758953703926467)
XLA Ops:
  9.8 410.1 %while.18 = (s32[]{:T(128)}, bf16[128,1536]{1,0:T(8,128)(2,1)S(1)}, bf16[128,768]{1,0:T(8,128)(2,1)}, bf16[8,128,1536]{2,1,0:T(8,128)(2,1)}, s32[]{:T(128)}, /*i...) while((s32[]{:T(128)}, bf16[128,1536]{1,0:T(8,128)(2,1)S(1)}, ...), condition=%wide.region_7.8_spmd, body=%wide.region_0.7_spmd.sunk | while | flops 1263716864 | bytes 21687792 | solution.py:103
  15.3 12.5 %collective-permute-done.1 = bf16[128,768]{1,0:T(8,128)(2,1)S(1)} collective-permute-done((bf16[128,768]{1,0:T(8,128)(2,1)}, bf16[128,768]{1,0:T(8,128)(2,1)S(1)}, u32[]{:S(2)}, u32[]{:S(2)}) %collective-permute-start.1) | collective-permute-done | bytes 196640 | tf_op jit(solution)/shard_map/while/body/eval_jaxpr/ppermute | solution.py:16
  34.0 11.6 %collective-permute-done.1 = bf16[128,768]{1,0:T(8,128)(2,1)S(1)} collective-permute-done((bf16[128,768]{1,0:T(8,128)(2,1)}, bf16[128,768]{1,0:T(8,128)(2,1)S(1)}, u32[]{:S(2)}, u32[]{:S(2)}) %collective-permute-start.1) | collective-permute-done | bytes 196640 | tf_op jit(solution)/shard_map/while/body/eval_jaxpr/ppermute | solution.py:16
  51.9 10.8 %collective-permute-done.1 = bf16[128,768]{1,0:T(8,128)(2,1)S(1)} collective-permute-done((bf16[128,768]{1,0:T(8,128)(2,1)}, bf16[128,768]{1,0:T(8,128)(2,1)S(1)}, u32[]{:S(2)}, u32[]{:S(2)}) %collective-permute-start.1) | collective-permute-done | bytes 196640 | tf_op jit(solution)/shard_map/while/body/eval_jaxpr/ppermute | solution.py:16
  68.9 9.9 %collective-permute-done.1 = bf16[128,768]{1,0:T(8,128)(2,1)S(1)} collective-permute-done((bf16[128,768]{1,0:T(8,128)(2,1)}, bf16[128,768]{1,0:T(8,128)(2,1)S(1)}, u32[]{:S(2)}, u32[]{:S(2)}) %collective-permute-start.1) | collective-permute-done | bytes 196640 | tf_op jit(solution)/shard_map/while/body/eval_jaxpr/ppermute | solution.py:16
  85.0 10.6 %collective-permute-done.1 = bf16[128,768]{1,0:T(8,128)(2,1)S(1)} collective-permute-done((bf16[128,768]{1,0:T(8,128)(2,1)}, bf16[128,768]{1,0:T(8,128)(2,1)S(1)}, u32[]{:S(2)}, u32[]{:S(2)}) %collective-permute-start.1) | collective-permute-done | bytes 196640 | tf_op jit(solution)/shard_map/while/body/eval_jaxpr/ppermute | solution.py:16
  101.8 10.3 %collective-permute-done.1 = bf16[128,768]{1,0:T(8,128)(2,1)S(1)} collective-permute-done((bf16[128,768]{1,0:T(8,128)(2,1)}, bf16[128,768]{1,0:T(8,128)(2,1)S(1)}, u32[]{:S(2)}, u32[]{:S(2)}) %collective-permute-start.1) | collective-permute-done | bytes 196640 | tf_op jit(solution)/shard_map/while/body/eval_jaxpr/ppermute | solution.py:16
  118.3 79.0 %collective-permute-done.1 = bf16[128,768]{1,0:T(8,128)(2,1)S(1)} collective-permute-done((bf16[128,768]{1,0:T(8,128)(2,1)}, bf16[128,768]{1,0:T(8,128)(2,1)S(1)}, u32[]{:S(2)}, u32[]{:S(2)}) %collective-permute-start.1) | collective-permute-done | bytes 196640 | tf_op jit(solution)/shard_map/while/body/eval_jaxpr/ppermute | solution.py:16
  199.0 10.8 %conditional.2 = ((bf16[128,1536]{1,0:T(8,128)(2,1)S(1)}, bf16[128,768]{1,0:T(8,128)(2,1)})) conditional(s32[]{:T(128)} %convert_element_type.92, (bf16[128,1536]{1,0:T(8,128)(2,1)S(1)}, bf16[128,768]{1,0:T(8,128)(2,1)}) %tuple.47, (bf16[128,1536]{1,0:T(8,128)(2,1)S(1)}, s32[]{:T(128)}, bf16[1,1536,768]{2,1,0:T(8,128)(2,1)}, f32[1]{0:T(128)}, ...), branch_computations={%region_1.1_spmd, %region_2.6_spmd} | conditional | flops 1263323648 | bytes 15789110 | solution.py:91
  214.3 9.7 %collective-permute-done.1 = bf16[128,768]{1,0:T(8,128)(2,1)S(1)} collective-permute-done((bf16[128,768]{1,0:T(8,128)(2,1)}, bf16[128,768]{1,0:T(8,128)(2,1)S(1)}, u32[]{:S(2)}, u32[]{:S(2)}) %collective-permute-start.1) | collective-permute-done | bytes 196640 | tf_op jit(solution)/shard_map/while/body/eval_jaxpr/ppermute | solution.py:16
  225.8 10.8 %conditional.2 = ((bf16[128,1536]{1,0:T(8,128)(2,1)S(1)}, bf16[128,768]{1,0:T(8,128)(2,1)})) conditional(s32[]{:T(128)} %convert_element_type.92, (bf16[128,1536]{1,0:T(8,128)(2,1)S(1)}, bf16[128,768]{1,0:T(8,128)(2,1)}) %tuple.47, (bf16[128,1536]{1,0:T(8,128)(2,1)S(1)}, s32[]{:T(128)}, bf16[1,1536,768]{2,1,0:T(8,128)(2,1)}, f32[1]{0:T(128)}, ...), branch_computations={%region_1.1_spmd, %region_2.6_spmd} | conditional | flops 1263323648 | bytes 15789110 | solution.py:91
  241.1 8.8 %collective-permute-done.1 = bf16[128,768]{1,0:T(8,128)(2,1)S(1)} collective-permute-done((bf16[128,768]{1,0:T(8,128)(2,1)}, bf16[128,768]{1,0:T(8,128)(2,1)S(1)}, u32[]{:S(2)}, u32[]{:S(2)}) %collective-permute-start.1) | collective-permute-done | bytes 196640 | tf_op jit(solution)/shard_map/while/body/eval_jaxpr/ppermute | solution.py:16
  251.6 10.8 %conditional.2 = ((bf16[128,1536]{1,0:T(8,128)(2,1)S(1)}, bf16[128,768]{1,0:T(8,128)(2,1)})) conditional(s32[]{:T(128)} %convert_element_type.92, (bf16[128,1536]{1,0:T(8,128)(2,1)S(1)}, bf16[128,768]{1,0:T(8,128)(2,1)}) %tuple.47, (bf16[128,1536]{1,0:T(8,128)(2,1)S(1)}, s32[]{:T(128)}, bf16[1,1536,768]{2,1,0:T(8,128)(2,1)}, f32[1]{0:T(128)}, ...), branch_computations={%region_1.1_spmd, %region_2.6_spmd} | conditional | flops 1263323648 | bytes 15789110 | solution.py:91
  277.2 10.8 %conditional.2 = ((bf16[128,1536]{1,0:T(8,128)(2,1)S(1)}, bf16[128,768]{1,0:T(8,128)(2,1)})) conditional(s32[]{:T(128)} %convert_element_type.92, (bf16[128,1536]{1,0:T(8,128)(2,1)S(1)}, bf16[128,768]{1,0:T(8,128)(2,1)}) %tuple.47, (bf16[128,1536]{1,0:T(8,128)(2,1)S(1)}, s32[]{:T(128)}, bf16[1,1536,768]{2,1,0:T(8,128)(2,1)}, f32[1]{0:T(128)}, ...), branch_computations={%region_1.1_spmd, %region_2.6_spmd} | conditional | flops 1263323648 | bytes 15789110 | solution.py:91
  292.5 9.1 %collective-permute-done.1 = bf16[128,768]{1,0:T(8,128)(2,1)S(1)} collective-permute-done((bf16[128,768]{1,0:T(8,128)(2,1)}, bf16[128,768]{1,0:T(8,128)(2,1)S(1)}, u32[]{:S(2)}, u32[]{:S(2)}) %collective-permute-start.1) | collective-permute-done | bytes 196640 | tf_op jit(solution)/shard_map/while/body/eval_jaxpr/ppermute | solution.py:16
  303.3 10.8 %conditional.2 = ((bf16[128,1536]{1,0:T(8,128)(2,1)S(1)}, bf16[128,768]{1,0:T(8,128)(2,1)})) conditional(s32[]{:T(128)} %convert_element_type.92, (bf16[128,1536]{1,0:T(8,128)(2,1)S(1)}, bf16[128,768]{1,0:T(8,128)(2,1)}) %tuple.47, (bf16[128,1536]{1,0:T(8,128)(2,1)S(1)}, s32[]{:T(128)}, bf16[1,1536,768]{2,1,0:T(8,128)(2,1)}, f32[1]{0:T(128)}, ...), branch_computations={%region_1.1_spmd, %region_2.6_spmd} | conditional | flops 1263323648 | bytes 15789110 | solution.py:91
  318.6 9.4 %collective-permute-done.1 = bf16[128,768]{1,0:T(8,128)(2,1)S(1)} collective-permute-done((bf16[128,768]{1,0:T(8,128)(2,1)}, bf16[128,768]{1,0:T(8,128)(2,1)S(1)}, u32[]{:S(2)}, u32[]{:S(2)}) %collective-permute-start.1) | collective-permute-done | bytes 196640 | tf_op jit(solution)/shard_map/while/body/eval_jaxpr/ppermute | solution.py:16
  329.7 10.8 %conditional.2 = ((bf16[128,1536]{1,0:T(8,128)(2,1)S(1)}, bf16[128,768]{1,0:T(8,128)(2,1)})) conditional(s32[]{:T(128)} %convert_element_type.92, (bf16[128,1536]{1,0:T(8,128)(2,1)S(1)}, bf16[128,768]{1,0:T(8,128)(2,1)}) %tuple.47, (bf16[128,1536]{1,0:T(8,128)(2,1)S(1)}, s32[]{:T(128)}, bf16[1,1536,768]{2,1,0:T(8,128)(2,1)}, f32[1]{0:T(128)}, ...), branch_computations={%region_1.1_spmd, %region_2.6_spmd} | conditional | flops 1263323648 | bytes 15789110 | solution.py:91
  345.0 9.4 %collective-permute-done.1 = bf16[128,768]{1,0:T(8,128)(2,1)S(1)} collective-permute-done((bf16[128,768]{1,0:T(8,128)(2,1)}, bf16[128,768]{1,0:T(8,128)(2,1)S(1)}, u32[]{:S(2)}, u32[]{:S(2)}) %collective-permute-start.1) | collective-permute-done | bytes 196640 | tf_op jit(solution)/shard_map/while/body/eval_jaxpr/ppermute | solution.py:16
  356.1 10.8 %conditional.2 = ((bf16[128,1536]{1,0:T(8,128)(2,1)S(1)}, bf16[128,768]{1,0:T(8,128)(2,1)})) conditional(s32[]{:T(128)} %convert_element_type.92, (bf16[128,1536]{1,0:T(8,128)(2,1)S(1)}, bf16[128,768]{1,0:T(8,128)(2,1)}) %tuple.47, (bf16[128,1536]{1,0:T(8,128)(2,1)S(1)}, s32[]{:T(128)}, bf16[1,1536,768]{2,1,0:T(8,128)(2,1)}, f32[1]{0:T(128)}, ...), branch_computations={%region_1.1_spmd, %region_2.6_spmd} | conditional | flops 1263323648 | bytes 15789110 | solution.py:91
  371.4 9.4 %collective-permute-done.1 = bf16[128,768]{1,0:T(8,128)(2,1)S(1)} collective-permute-done((bf16[128,768]{1,0:T(8,128)(2,1)}, bf16[128,768]{1,0:T(8,128)(2,1)S(1)}, u32[]{:S(2)}, u32[]{:S(2)}) %collective-permute-start.1) | collective-permute-done | bytes 196640 | tf_op jit(solution)/shard_map/while/body/eval_jaxpr/ppermute | solution.py:16
  382.6 10.8 %conditional.2 = ((bf16[128,1536]{1,0:T(8,128)(2,1)S(1)}, bf16[128,768]{1,0:T(8,128)(2,1)})) conditional(s32[]{:T(128)} %convert_element_type.92, (bf16[128,1536]{1,0:T(8,128)(2,1)S(1)}, bf16[128,768]{1,0:T(8,128)(2,1)}) %tuple.47, (bf16[128,1536]{1,0:T(8,128)(2,1)S(1)}, s32[]{:T(128)}, bf16[1,1536,768]{2,1,0:T(8,128)(2,1)}, f32[1]{0:T(128)}, ...), branch_computations={%region_1.1_spmd, %region_2.6_spmd} | conditional | flops 1263323648 | bytes 15789110 | solution.py:91
  397.9 21.4 %collective-permute-done.1 = bf16[128,768]{1,0:T(8,128)(2,1)S(1)} collective-permute-done((bf16[128,768]{1,0:T(8,128)(2,1)}, bf16[128,768]{1,0:T(8,128)(2,1)S(1)}, u32[]{:S(2)}, u32[]{:S(2)}) %collective-permute-start.1) | collective-permute-done | bytes 196640 | tf_op jit(solution)/shard_map/while/body/eval_jaxpr/ppermute | solution.py:16
  419.9 25.5 %all_to_all.5 = bf16[8,128,1536]{2,1,0:T(8,128)(2,1)S(1)} all-to-all(bf16[8,128,1536]{2,1,0:T(8,128)(2,1)} %get-tuple-element.271), channel_id=1, replica_groups=mesh['section'=8,'dp'=32] {'section'}, dimensions={0} | all-to-all | bytes 6291456 | tf_op jit(solution)/shard_map/all_to_all | solution.py:106
  (207 shorter events, 192.5 us)
Async XLA Ops:
  10.8 17.6 %collective-permute-start = (bf16[128,1536]{1,0:T(8,128)(2,1)S(1)}, bf16[128,1536]{1,0:T(8,128)(2,1)S(1)}, u32[]{:S(2)}, u32[]{:S(2)}) collective-permute-start(bf16[128,1536]{1,0:T(8,128)(2,1)S(1)} %get-tuple-element.413), channel_id=1, source_target_pairs={{0,32},{32,64},{64,96},{96,128},{128,160},{160,192},{192,224},{1,3... | collective-permute-start | bytes 1179656 | tf_op jit(solution)/shard_map/while/body/eval_jaxpr/ppermute | solution.py:16
  12.1 15.7 %collective-permute-start.1 = (bf16[128,768]{1,0:T(8,128)(2,1)}, bf16[128,768]{1,0:T(8,128)(2,1)S(1)}, u32[]{:S(2)}, u32[]{:S(2)}) collective-permute-start(bf16[128,768]{1,0:T(8,128)(2,1)} %get-tuple-element.414), channel_id=1, source_target_pairs={{0,32},{32,64},{64,96},{96,128},{128,160},{160,192},{192,224},{1,3... | collective-permute-start | bytes 589832 | tf_op jit(solution)/shard_map/while/body/eval_jaxpr/ppermute | solution.py:16
  29.6 16.8 %collective-permute-start = (bf16[128,1536]{1,0:T(8,128)(2,1)S(1)}, bf16[128,1536]{1,0:T(8,128)(2,1)S(1)}, u32[]{:S(2)}, u32[]{:S(2)}) collective-permute-start(bf16[128,1536]{1,0:T(8,128)(2,1)S(1)} %get-tuple-element.413), channel_id=1, source_target_pairs={{0,32},{32,64},{64,96},{96,128},{128,160},{160,192},{192,224},{1,3... | collective-permute-start | bytes 1179656 | tf_op jit(solution)/shard_map/while/body/eval_jaxpr/ppermute | solution.py:16
  30.9 14.8 %collective-permute-start.1 = (bf16[128,768]{1,0:T(8,128)(2,1)}, bf16[128,768]{1,0:T(8,128)(2,1)S(1)}, u32[]{:S(2)}, u32[]{:S(2)}) collective-permute-start(bf16[128,768]{1,0:T(8,128)(2,1)} %get-tuple-element.414), channel_id=1, source_target_pairs={{0,32},{32,64},{64,96},{96,128},{128,160},{160,192},{192,224},{1,3... | collective-permute-start | bytes 589832 | tf_op jit(solution)/shard_map/while/body/eval_jaxpr/ppermute | solution.py:16
  47.4 15.9 %collective-permute-start = (bf16[128,1536]{1,0:T(8,128)(2,1)S(1)}, bf16[128,1536]{1,0:T(8,128)(2,1)S(1)}, u32[]{:S(2)}, u32[]{:S(2)}) collective-permute-start(bf16[128,1536]{1,0:T(8,128)(2,1)S(1)} %get-tuple-element.413), channel_id=1, source_target_pairs={{0,32},{32,64},{64,96},{96,128},{128,160},{160,192},{192,224},{1,3... | collective-permute-start | bytes 1179656 | tf_op jit(solution)/shard_map/while/body/eval_jaxpr/ppermute | solution.py:16
  48.7 14.0 %collective-permute-start.1 = (bf16[128,768]{1,0:T(8,128)(2,1)}, bf16[128,768]{1,0:T(8,128)(2,1)S(1)}, u32[]{:S(2)}, u32[]{:S(2)}) collective-permute-start(bf16[128,768]{1,0:T(8,128)(2,1)} %get-tuple-element.414), channel_id=1, source_target_pairs={{0,32},{32,64},{64,96},{96,128},{128,160},{160,192},{192,224},{1,3... | collective-permute-start | bytes 589832 | tf_op jit(solution)/shard_map/while/body/eval_jaxpr/ppermute | solution.py:16
  64.4 15.1 %collective-permute-start = (bf16[128,1536]{1,0:T(8,128)(2,1)S(1)}, bf16[128,1536]{1,0:T(8,128)(2,1)S(1)}, u32[]{:S(2)}, u32[]{:S(2)}) collective-permute-start(bf16[128,1536]{1,0:T(8,128)(2,1)S(1)} %get-tuple-element.413), channel_id=1, source_target_pairs={{0,32},{32,64},{64,96},{96,128},{128,160},{160,192},{192,224},{1,3... | collective-permute-start | bytes 1179656 | tf_op jit(solution)/shard_map/while/body/eval_jaxpr/ppermute | solution.py:16
  65.7 13.1 %collective-permute-start.1 = (bf16[128,768]{1,0:T(8,128)(2,1)}, bf16[128,768]{1,0:T(8,128)(2,1)S(1)}, u32[]{:S(2)}, u32[]{:S(2)}) collective-permute-start(bf16[128,768]{1,0:T(8,128)(2,1)} %get-tuple-element.414), channel_id=1, source_target_pairs={{0,32},{32,64},{64,96},{96,128},{128,160},{160,192},{192,224},{1,3... | collective-permute-start | bytes 589832 | tf_op jit(solution)/shard_map/while/body/eval_jaxpr/ppermute | solution.py:16
  80.5 15.7 %collective-permute-start = (bf16[128,1536]{1,0:T(8,128)(2,1)S(1)}, bf16[128,1536]{1,0:T(8,128)(2,1)S(1)}, u32[]{:S(2)}, u32[]{:S(2)}) collective-permute-start(bf16[128,1536]{1,0:T(8,128)(2,1)S(1)} %get-tuple-element.413), channel_id=1, source_target_pairs={{0,32},{32,64},{64,96},{96,128},{128,160},{160,192},{192,224},{1,3... | collective-permute-start | bytes 1179656 | tf_op jit(solution)/shard_map/while/body/eval_jaxpr/ppermute | solution.py:16
  81.8 13.7 %collective-permute-start.1 = (bf16[128,768]{1,0:T(8,128)(2,1)}, bf16[128,768]{1,0:T(8,128)(2,1)S(1)}, u32[]{:S(2)}, u32[]{:S(2)}) collective-permute-start(bf16[128,768]{1,0:T(8,128)(2,1)} %get-tuple-element.414), channel_id=1, source_target_pairs={{0,32},{32,64},{64,96},{96,128},{128,160},{160,192},{192,224},{1,3... | collective-permute-start | bytes 589832 | tf_op jit(solution)/shard_map/while/body/eval_jaxpr/ppermute | solution.py:16
  97.3 15.5 %collective-permute-start = (bf16[128,1536]{1,0:T(8,128)(2,1)S(1)}, bf16[128,1536]{1,0:T(8,128)(2,1)S(1)}, u32[]{:S(2)}, u32[]{:S(2)}) collective-permute-start(bf16[128,1536]{1,0:T(8,128)(2,1)S(1)} %get-tuple-element.413), channel_id=1, source_target_pairs={{0,32},{32,64},{64,96},{96,128},{128,160},{160,192},{192,224},{1,3... | collective-permute-start | bytes 1179656 | tf_op jit(solution)/shard_map/while/body/eval_jaxpr/ppermute | solution.py:16
  98.6 13.5 %collective-permute-start.1 = (bf16[128,768]{1,0:T(8,128)(2,1)}, bf16[128,768]{1,0:T(8,128)(2,1)S(1)}, u32[]{:S(2)}, u32[]{:S(2)}) collective-permute-start(bf16[128,768]{1,0:T(8,128)(2,1)} %get-tuple-element.414), channel_id=1, source_target_pairs={{0,32},{32,64},{64,96},{96,128},{128,160},{160,192},{192,224},{1,3... | collective-permute-start | bytes 589832 | tf_op jit(solution)/shard_map/while/body/eval_jaxpr/ppermute | solution.py:16
  113.8 84.1 %collective-permute-start = (bf16[128,1536]{1,0:T(8,128)(2,1)S(1)}, bf16[128,1536]{1,0:T(8,128)(2,1)S(1)}, u32[]{:S(2)}, u32[]{:S(2)}) collective-permute-start(bf16[128,1536]{1,0:T(8,128)(2,1)S(1)} %get-tuple-element.413), channel_id=1, source_target_pairs={{0,32},{32,64},{64,96},{96,128},{128,160},{160,192},{192,224},{1,3... | collective-permute-start | bytes 1179656 | tf_op jit(solution)/shard_map/while/body/eval_jaxpr/ppermute | solution.py:16
  115.1 82.2 %collective-permute-start.1 = (bf16[128,768]{1,0:T(8,128)(2,1)}, bf16[128,768]{1,0:T(8,128)(2,1)S(1)}, u32[]{:S(2)}, u32[]{:S(2)}) collective-permute-start(bf16[128,768]{1,0:T(8,128)(2,1)} %get-tuple-element.414), channel_id=1, source_target_pairs={{0,32},{32,64},{64,96},{96,128},{128,160},{160,192},{192,224},{1,3... | collective-permute-start | bytes 589832 | tf_op jit(solution)/shard_map/while/body/eval_jaxpr/ppermute | solution.py:16
  209.8 14.9 %collective-permute-start = (bf16[128,1536]{1,0:T(8,128)(2,1)S(1)}, bf16[128,1536]{1,0:T(8,128)(2,1)S(1)}, u32[]{:S(2)}, u32[]{:S(2)}) collective-permute-start(bf16[128,1536]{1,0:T(8,128)(2,1)S(1)} %get-tuple-element.413), channel_id=1, source_target_pairs={{0,32},{32,64},{64,96},{96,128},{128,160},{160,192},{192,224},{1,3... | collective-permute-start | bytes 1179656 | tf_op jit(solution)/shard_map/while/body/eval_jaxpr/ppermute | solution.py:16
  211.1 12.9 %collective-permute-start.1 = (bf16[128,768]{1,0:T(8,128)(2,1)}, bf16[128,768]{1,0:T(8,128)(2,1)S(1)}, u32[]{:S(2)}, u32[]{:S(2)}) collective-permute-start(bf16[128,768]{1,0:T(8,128)(2,1)} %get-tuple-element.414), channel_id=1, source_target_pairs={{0,32},{32,64},{64,96},{96,128},{128,160},{160,192},{192,224},{1,3... | collective-permute-start | bytes 589832 | tf_op jit(solution)/shard_map/while/body/eval_jaxpr/ppermute | solution.py:16
  236.6 14.0 %collective-permute-start = (bf16[128,1536]{1,0:T(8,128)(2,1)S(1)}, bf16[128,1536]{1,0:T(8,128)(2,1)S(1)}, u32[]{:S(2)}, u32[]{:S(2)}) collective-permute-start(bf16[128,1536]{1,0:T(8,128)(2,1)S(1)} %get-tuple-element.413), channel_id=1, source_target_pairs={{0,32},{32,64},{64,96},{96,128},{128,160},{160,192},{192,224},{1,3... | collective-permute-start | bytes 1179656 | tf_op jit(solution)/shard_map/while/body/eval_jaxpr/ppermute | solution.py:16
  262.4 13.7 %collective-permute-start = (bf16[128,1536]{1,0:T(8,128)(2,1)S(1)}, bf16[128,1536]{1,0:T(8,128)(2,1)S(1)}, u32[]{:S(2)}, u32[]{:S(2)}) collective-permute-start(bf16[128,1536]{1,0:T(8,128)(2,1)S(1)} %get-tuple-element.413), channel_id=1, source_target_pairs={{0,32},{32,64},{64,96},{96,128},{128,160},{160,192},{192,224},{1,3... | collective-permute-start | bytes 1179656 | tf_op jit(solution)/shard_map/while/body/eval_jaxpr/ppermute | solution.py:16
  288.0 14.3 %collective-permute-start = (bf16[128,1536]{1,0:T(8,128)(2,1)S(1)}, bf16[128,1536]{1,0:T(8,128)(2,1)S(1)}, u32[]{:S(2)}, u32[]{:S(2)}) collective-permute-start(bf16[128,1536]{1,0:T(8,128)(2,1)S(1)} %get-tuple-element.413), channel_id=1, source_target_pairs={{0,32},{32,64},{64,96},{96,128},{128,160},{160,192},{192,224},{1,3... | collective-permute-start | bytes 1179656 | tf_op jit(solution)/shard_map/while/body/eval_jaxpr/ppermute | solution.py:16
  314.1 14.6 %collective-permute-start = (bf16[128,1536]{1,0:T(8,128)(2,1)S(1)}, bf16[128,1536]{1,0:T(8,128)(2,1)S(1)}, u32[]{:S(2)}, u32[]{:S(2)}) collective-permute-start(bf16[128,1536]{1,0:T(8,128)(2,1)S(1)} %get-tuple-element.413), channel_id=1, source_target_pairs={{0,32},{32,64},{64,96},{96,128},{128,160},{160,192},{192,224},{1,3... | collective-permute-start | bytes 1179656 | tf_op jit(solution)/shard_map/while/body/eval_jaxpr/ppermute | solution.py:16
  340.5 14.6 %collective-permute-start = (bf16[128,1536]{1,0:T(8,128)(2,1)S(1)}, bf16[128,1536]{1,0:T(8,128)(2,1)S(1)}, u32[]{:S(2)}, u32[]{:S(2)}) collective-permute-start(bf16[128,1536]{1,0:T(8,128)(2,1)S(1)} %get-tuple-element.413), channel_id=1, source_target_pairs={{0,32},{32,64},{64,96},{96,128},{128,160},{160,192},{192,224},{1,3... | collective-permute-start | bytes 1179656 | tf_op jit(solution)/shard_map/while/body/eval_jaxpr/ppermute | solution.py:16
  366.9 14.6 %collective-permute-start = (bf16[128,1536]{1,0:T(8,128)(2,1)S(1)}, bf16[128,1536]{1,0:T(8,128)(2,1)S(1)}, u32[]{:S(2)}, u32[]{:S(2)}) collective-permute-start(bf16[128,1536]{1,0:T(8,128)(2,1)S(1)} %get-tuple-element.413), channel_id=1, source_target_pairs={{0,32},{32,64},{64,96},{96,128},{128,160},{160,192},{192,224},{1,3... | collective-permute-start | bytes 1179656 | tf_op jit(solution)/shard_map/while/body/eval_jaxpr/ppermute | solution.py:16
  393.4 26.6 %collective-permute-start = (bf16[128,1536]{1,0:T(8,128)(2,1)S(1)}, bf16[128,1536]{1,0:T(8,128)(2,1)S(1)}, u32[]{:S(2)}, u32[]{:S(2)}) collective-permute-start(bf16[128,1536]{1,0:T(8,128)(2,1)S(1)} %get-tuple-element.413), channel_id=1, source_target_pairs={{0,32},{32,64},{64,96},{96,128},{128,160},{160,192},{192,224},{1,3... | collective-permute-start | bytes 1179656 | tf_op jit(solution)/shard_map/while/body/eval_jaxpr/ppermute | solution.py:16
  394.7 24.6 %collective-permute-start.1 = (bf16[128,768]{1,0:T(8,128)(2,1)}, bf16[128,768]{1,0:T(8,128)(2,1)S(1)}, u32[]{:S(2)}, u32[]{:S(2)}) collective-permute-start(bf16[128,768]{1,0:T(8,128)(2,1)} %get-tuple-element.414), channel_id=1, source_target_pairs={{0,32},{32,64},{64,96},{96,128},{128,160},{160,192},{192,224},{1,3... | collective-permute-start | bytes 589832 | tf_op jit(solution)/shard_map/while/body/eval_jaxpr/ppermute | solution.py:16
  (6 other events, 73.8 us)
where the time goes:
time: 451 us; the launch traced here: 446 us
  waiting for transfers between devices  230 us (51%)
  matrix products  77.9 us (17%)
  starting transfers between devices  38.8 us (9%)
  local copies, waits for them, and re-layouts  37.4 us (8%)
  other arithmetic  29.8 us (7%)
  blocking collectives  25.5 us (6%)
  loops' own time  6.42 us (1%)
    ppermute x30, waiting for transfers between devices, shifted(): lax.ppermute(value, axis, [(source, source + steps) for source in range(f...  230 us
    dot_general x32, matrix products, project(): return jnp.dot(normed, weight, preferred_element_type=jnp.float32)  73.8 us
    ppermute x30, starting transfers between devices, shifted(): lax.ppermute(value, axis, [(source, source + steps) for source in range(f...  38.8 us
    all_to_all x1, blocking collectives, body(): lax.all_to_all(outputs, 'section', split_axis=0, concat_axis=0, tiled=True)  25.5 us
    select_n x15, other arithmetic, advance(): hidden = jnp.where(section_index == 0, fresh_rows, received)  15.6 us
    dynamic_slice x15, local copies, waits for them, and re-layouts, advance(): previous = lax.dynamic_index_in_dim(outputs, slot_index, 0, keepdims=False)  15.4 us
    dynamic_update_slice x15, other arithmetic, advance(): outputs = lax.dynamic_update_index_in_dim(outputs, finished, slot_index, 0)  12.6 us
    while x15, local copies, waits for them, and re-layouts  10.2 us
  transfers between devices with their start and end apart: 30, of which 15 were waited for; matrix products, arithmetic and copies ran while one was open for 9% of the time, Pallas kernels for 0%

commit v1 on v0

v1 whole, which is shorter than its diff:
```python
import functools

import jax
import jax.numpy as jnp
from jax import lax
from jax.experimental import pallas as pl
from jax.experimental.pallas import tpu as pltpu
from jax.sharding import PartitionSpec as P

MESH = pl.DeviceIdType.MESH
HEADS = 6
ROWS = 32
LEAD = {3: 9, 2: 4}

epsilon = 1e-06
score_scale = 0.12


def inverse_norm(tensor):
    return lax.rsqrt(jnp.mean(tensor * tensor, axis=-1, keepdims=True) + epsilon)


def kernel(
    sections,
    x_hbm,
    wq_hbm,
    wk_hbm,
    wv_hbm,
    wo_hbm,
    mix_ref,
    out_hbm,
    wq,
    wk,
    wv,
    wo,
    arrived,
    leaving,
    first,
    key_cache,
    value_cache,
    result,
    weight_sem,
    arrive_sem,
    leave_sem,
    first_sem,
    first_y_sem,
    first_z_sem,
    result_sem,
    out_sem,
):
    me = lax.axis_index("section")
    last = sections - 1
    half = sections // 2
    micro, seq, width = x_hbm.shape
    head_dim = wq.shape[1] // HEADS
    cuts = seq // ROWS
    pieces = micro * cuts
    bf16 = jnp.bfloat16

    weight_copies = [
        pltpu.make_async_copy(source.at[0], target, weight_sem.at[n])
        for n, (source, target) in enumerate(
            ((wq_hbm, wq), (wk_hbm, wk), (wv_hbm, wv), (wo_hbm, wo))
        )
    ]

    def input_copy(index):
        rows = pl.ds(pl.multiple_of(lax.rem(index, cuts) * ROWS, ROWS), ROWS)
        return pltpu.make_async_copy(
            x_hbm.at[index // cuts, rows], arrived.at[index], arrive_sem.at[index]
        )

    def hidden_copy(index):
        return pltpu.make_async_remote_copy(
            src_ref=leaving.at[index],
            dst_ref=arrived.at[index],
            send_sem=leave_sem.at[index],
            recv_sem=arrive_sem.at[index],
            device_id={"section": lax.rem(me + 1, sections)},
            device_id_type=MESH,
        )

    def result_copy(index):
        return pltpu.make_async_remote_copy(
            src_ref=leaving.at[index],
            dst_ref=result.at[lax.rem(index, cuts)],
            send_sem=leave_sem.at[index],
            recv_sem=result_sem.at[lax.rem(index, cuts)],
            device_id={"section": index // cuts},
            device_id_type=MESH,
        )

    def first_along_y(index):
        target = jnp.where(me == 0, half - 1, me - 1)
        return pltpu.make_async_remote_copy(
            src_ref=first.at[index],
            dst_ref=first.at[index],
            send_sem=first_y_sem.at[index],
            recv_sem=first_sem.at[index],
            device_id={"section": target},
            device_id_type=MESH,
        )

    def first_along_z(index):
        return pltpu.make_async_remote_copy(
            src_ref=first.at[index],
            dst_ref=first.at[index],
            send_sem=first_z_sem.at[index],
            recv_sem=first_sem.at[index],
            device_id={"section": lax.rem(me + half, sections)},
            device_id_type=MESH,
        )

    @pl.when(me == 0)
    def _():
        input_copy(0).start()

    for copy in weight_copies:
        copy.start()

    @pl.when(me == 0)
    def _():
        @pl.loop(1, pieces)
        def _(index):
            input_copy(index).start()

    barrier = pltpu.get_barrier_semaphore()
    for step in range(1, sections):
        pl.semaphore_signal(
            barrier,
            inc=1,
            device_id={"section": lax.rem(me + step, sections)},
            device_id_type=MESH,
        )
    key_cache[...] = jnp.zeros_like(key_cache)
    value_cache[...] = jnp.zeros_like(value_cache)
    pl.semaphore_wait(barrier, sections - 1)
    for copy in weight_copies:
        copy.wait()

    passes_on = jnp.logical_and(me >= 2, me < half)
    lead = jnp.where(me == 3, LEAD[3], LEAD[2])

    def pass_on(index):
        first_along_y(index).wait_recv()
        first_along_y(index).start()

    @pl.when(passes_on)
    def _():
        @pl.loop(0, lead)
        def _(index):
            pass_on(index)

    share = jnp.where(me == 0, 1.0, mix_ref[0])

    @pl.loop(0, pieces)
    def _(index):
        cut = lax.rem(index, cuts)
        start = pl.multiple_of(cut * ROWS, ROWS)
        rows = pl.ds(start, ROWS)

        input_copy(index).wait()

        hidden = arrived[index].astype(jnp.float32)
        normed = (hidden * inverse_norm(hidden)).astype(bf16)
        queries = jnp.dot(normed, wq[...], preferred_element_type=jnp.float32)
        keys = jnp.dot(normed, wk[...], preferred_element_type=jnp.float32)
        values = jnp.dot(normed, wv[...], preferred_element_type=jnp.float32)

        @pl.when(me == 0)
        def _():
            first[index] = values.astype(bf16)
            first_along_y(index).start()

        @pl.when(jnp.logical_or(me == 1, me >= half))
        def _():
            first_along_y(index).wait_recv()

        @pl.when(jnp.logical_and(passes_on, index + lead < pieces))
        def _():
            pass_on(index + lead)

        @pl.when(me < half)
        def _():
            first_along_z(index).start()

        used = share * values + (1.0 - share) * first[index].astype(jnp.float32)
        value_cache[rows, :] = used.astype(bf16)

        heads = [slice(n * head_dim, (n + 1) * head_dim) for n in range(HEADS)]
        for head in heads:
            part = keys[:, head]
            key_cache[rows, head] = (part * inverse_norm(part)).astype(bf16)
        query_parts = []
        for head in heads:
            part = queries[:, head]
            query_parts.append((part * inverse_norm(part)).astype(bf16))
        query_at = start + lax.broadcasted_iota(jnp.int32, (ROWS, seq), 0)
        key_at = lax.broadcasted_iota(jnp.int32, (ROWS, seq), 1)
        causal = query_at >= key_at
        probabilities = []
        for head, part in zip(heads, query_parts):
            scores = score_scale * lax.dot_general(
                part,
                key_cache[:, head],
                (((1,), (1,)), ((), ())),
                preferred_element_type=jnp.float32,
            )
            weights = jnp.where(causal, jnp.exp(scores), 0.0)
            total = jnp.sum(weights, axis=-1, keepdims=True)
            probabilities.append((weights * (1.0 / total)).astype(bf16))
        attended = jnp.concatenate(
            [
                jnp.dot(
                    part, value_cache[:, head], preferred_element_type=jnp.float32
                ).astype(bf16)
                for head, part in zip(heads, probabilities)
            ],
            axis=1,
        )
        added = jnp.dot(attended, wo[...], preferred_element_type=jnp.float32)
        following = (hidden + added).astype(bf16)
        leaving[index] = following

        @pl.when(me < last)
        def _():
            hidden_copy(index).start()

        @pl.when(me == last)
        def _():
            @pl.when(index // cuts < last)
            def _():
                result_copy(index).start()

            @pl.when(index // cuts == last)
            def _():
                result[cut] = following

    @pl.when(me < last)
    def _():
        @pl.loop(0, cuts)
        def _(index):
            result_copy(index).wait_recv()

    out_copies = [
        pltpu.make_async_copy(
            result.at[n], out_hbm.at[0, pl.ds(n * ROWS, ROWS)], out_sem.at[n]
        )
        for n in range(cuts)
    ]
    for copy in out_copies:
        copy.start()

    @pl.loop(0, pieces)
    def _(index):
        @pl.when(jnp.logical_or(me < last, index // cuts < last))
        def _():
            hidden_copy(index).wait_send()

        @pl.when(jnp.logical_or(me == 0, passes_on))
        def _():
            first_along_y(index).wait_send()

        @pl.when(me < half)
        def _():
            first_along_z(index).wait_send()

    for copy in out_copies:
        copy.wait()


def body(inputs, w_query, w_key, w_value, w_out, mixing):
    sections = lax.axis_size("section")
    micro, seq, width = inputs.shape
    inner = w_query.shape[2]
    cuts = seq // ROWS
    pieces = micro * cuts
    anywhere = pl.BlockSpec(memory_space=pl.ANY)
    dma = pltpu.SemaphoreType.DMA
    return pl.pallas_call(
        functools.partial(kernel, sections),
        out_shape=jax.ShapeDtypeStruct((micro // sections, seq, width), jnp.bfloat16),
        in_specs=[anywhere] * 5 + [pl.BlockSpec(memory_space=pltpu.SMEM)],
        out_specs=anywhere,
        scratch_shapes=[
            pltpu.VMEM((width, inner), jnp.bfloat16),
            pltpu.VMEM((width, inner), jnp.bfloat16),
            pltpu.VMEM((width, inner), jnp.bfloat16),
            pltpu.VMEM((inner, width), jnp.bfloat16),
            pltpu.VMEM((pieces, ROWS, width), jnp.bfloat16),
            pltpu.VMEM((pieces, ROWS, width), jnp.bfloat16),
            pltpu.VMEM((pieces, ROWS, inner), jnp.bfloat16),
            pltpu.VMEM((seq, inner), jnp.bfloat16),
            pltpu.VMEM((seq, inner), jnp.bfloat16),
            pltpu.VMEM((cuts, ROWS, width), jnp.bfloat16),
            dma((4,)),
            dma((pieces,)),
            dma((pieces,)),
            dma((pieces,)),
            dma((pieces,)),
            dma((pieces,)),
            dma((cuts,)),
            dma((cuts,)),
        ],
        compiler_params=pltpu.CompilerParams(
            collective_id=0, has_side_effects=True, vmem_limit_bytes=60 * 2**20
        ),
    )(inputs, w_query, w_key, w_value, w_out, mixing)


def solution(mesh):
    in_specs = (
        P("dp", None, None),
        P("section", None, None),
        P("section", None, None),
        P("section", None, None),
        P("section", None, None),
        P("section"),
    )
    out_specs = P(("dp", "section"), None, None)
    return jax.shard_map(body, mesh=mesh, in_specs=in_specs, out_specs=out_specs, check_vma=False)
```

time: 451 us -> 161 us (0.36); the launches traced: 446 us -> 161 us
  waiting for transfers between devices: 230 us -> 0 us
  Pallas kernels: 0 us -> 159 us
  matrix products: 77.9 us -> 0 us
  starting transfers between devices: 38.8 us -> 0 us
  local copies, waits for them, and re-layouts: 37.4 us -> 1.77 us
  other arithmetic: 29.8 us -> 0 us
  blocking collectives: 25.5 us -> 0 us
  loops' own time: 6.42 us -> 0 us
    ppermute x30 -> x0, waiting for transfers between devices: 230 us -> none  [shifted(): lax.ppermute(value, axis, [(source, source + steps) for source in range(f...]
    pallas_call x0 -> x1, Pallas kernels: none -> 159 us  [body(): pl.pallas_call(functools.partial(kernel, sections), out_shape=jax.ShapeDt...]
    dot_general x48 -> x0, matrix products: 77.9 us -> none  [the longest x32 73.8 us: project(): return jnp.dot(normed, weight, preferred_element_type=jnp.float32)]
    ppermute x30 -> x0, starting transfers between devices: 38.8 us -> none  [shifted(): lax.ppermute(value, axis, [(source, source + steps) for source in range(f...]
    all_to_all x1 -> x0, blocking collectives: 25.5 us -> none  [body(): lax.all_to_all(outputs, 'section', split_axis=0, concat_axis=0, tiled=True)]
    while x17 -> x0, local copies, waits for them, and re-layouts: 17.3 us -> none
    select_n x15 -> x0, other arithmetic: 15.6 us -> none  [advance(): hidden = jnp.where(section_index == 0, fresh_rows, received)]
    dynamic_slice x15 -> x0, local copies, waits for them, and re-layouts: 15.4 us -> none  [advance(): previous = lax.dynamic_index_in_dim(outputs, slot_index, 0, keepdims=False)]
  transfers between devices with their start and end apart: 30 -> 0, of which waited for: 15 -> 0; matrix products, arithmetic and copies ran while one was open for 9% -> 0% of each run, Pallas kernels for 0% -> 0%
where the time goes in v1:
time: 161 us
  Pallas kernels  159 us (99%)
  local copies, waits for them, and re-layouts  1.77 us (1%)
    pallas_call x1, Pallas kernels, body(): pl.pallas_call(functools.partial(kernel, sections), out_shape=jax.ShapeDt...  159 us

profile of v1, /device:TPU:184, one launch (start us, length us, event | category | flops | bytes accessed | tf_op | source)
XLA Modules:
  0.0 161.1 jit_solution(11135705780640423181)
XLA Ops:
  0.7 158.7 %shard_map.64 = bf16[1,128,1536]{2,1,0:T(8,128)(2,1)} custom-call(bf16[8,128,1536]{2,1,0:T(8,128)(2,1)} %x_hbm.1, bf16[1,1536,768]{2,1,0:T(8,128)(2,1)} %wq_hbm.1, bf16[1,1536,768]{2,1,0:T(8,128)(2,1)} %wk_hbm.1, bf16[1,1536,768]{2,1,0:T(8,128)(2,1)} %wv_hbm.1, bf16[1,768,1536]{2,1,0:T(8,128)(2,1)} %wo_hbm.1, f32[1]{0:T(128)S(6)} %copy.8.mix_ref), custom_call_target="tpu_custom_call" | custom-call | tf_op jit(solution)/shard_map/pallas_call | solution.py:280
  159.3 1.8 %copy.9 = bf16[1,128,1536]{2,1,0:T(8,128)(2,1)} copy(bf16[1,128,1536]{2,1,0:T(8,128)(2,1)} %shard_map.64) | data formatting | bytes 786432

commit v2 on v1

--- a/solution.py
+++ b/solution.py
@@ -10,7 +10,8 @@
 MESH = pl.DeviceIdType.MESH
 HEADS = 6
 ROWS = 32
-LEAD = {3: 9, 2: 4}
+LEAD = {3: 14, 2: 5}
+DIRECT = 2
 
 epsilon = 1e-06
 score_scale = 0.12
@@ -45,6 +46,7 @@
     first_sem,
     first_y_sem,
     first_z_sem,
+    first_direct_sem,
     result_sem,
     out_sem,
 ):
@@ -60,7 +62,7 @@
     weight_copies = [
         pltpu.make_async_copy(source.at[0], target, weight_sem.at[n])
         for n, (source, target) in enumerate(
-            ((wq_hbm, wq), (wk_hbm, wk), (wv_hbm, wv), (wo_hbm, wo))
+            ((wv_hbm, wv), (wq_hbm, wq), (wk_hbm, wk), (wo_hbm, wo))
         )
     ]
 
@@ -91,7 +93,7 @@
         )
 
     def first_along_y(index):
-        target = jnp.where(me == 0, half - 1, me - 1)
+        target = jnp.where(me % half == 0, me + half - 1, me - 1)
         return pltpu.make_async_remote_copy(
             src_ref=first.at[index],
             dst_ref=first.at[index],
@@ -111,16 +113,27 @@
             device_id_type=MESH,
         )
 
+    def first_direct(index):
+        return pltpu.make_async_remote_copy(
+            src_ref=first.at[index],
+            dst_ref=first.at[index],
+            send_sem=first_direct_sem.at[index],
+            recv_sem=first_sem.at[index],
+            device_id={"section": 1},
+            device_id_type=MESH,
+        )
+
     @pl.when(me == 0)
     def _():
-        input_copy(0).start()
+        for n in range(cuts):
+            input_copy(n).start()
 
     for copy in weight_copies:
         copy.start()
 
     @pl.when(me == 0)
     def _():
-        @pl.loop(1, pieces)
+        @pl.loop(cuts, pieces)
         def _(index):
             input_copy(index).start()
 
@@ -135,106 +148,189 @@
     key_cache[...] = jnp.zeros_like(key_cache)
     value_cache[...] = jnp.zeros_like(value_cache)
     pl.semaphore_wait(barrier, sections - 1)
-    for copy in weight_copies:
-        copy.wait()
-
+
+    f32 = jnp.float32
     passes_on = jnp.logical_and(me >= 2, me < half)
-    lead = jnp.where(me == 3, LEAD[3], LEAD[2])
+    lead = jnp.where(me == half - 1, LEAD[3], LEAD[2])
+    share = mix_ref[0]
 
     def pass_on(index):
         first_along_y(index).wait_recv()
-        first_along_y(index).start()
-
-    @pl.when(passes_on)
-    def _():
-        @pl.loop(0, lead)
-        def _(index):
-            pass_on(index)
-
-    share = jnp.where(me == 0, 1.0, mix_ref[0])
-
-    @pl.loop(0, pieces)
-    def _(index):
+
+        @pl.when(jnp.logical_or(me == half - 1, index >= DIRECT))
+        def _():
+            first_along_y(index).start()
+
+        @pl.when(me == 2)
+        def _():
+            first_along_z(index).start()
+
+    def make_first(sequence):
+        base = sequence * cuts
+        for n in range(cuts):
+            input_copy(base + n).wait()
+        packed = jnp.concatenate([arrived[base + n] for n in range(cuts)], axis=0)
+        scale = inverse_norm(packed.astype(f32))
+        values = scale * jnp.dot(packed, wv[...], preferred_element_type=f32)
+        for n in range(cuts):
+            first[base + n] = values[n * ROWS : (n + 1) * ROWS].astype(bf16)
+        for n in range(cuts):
+            first_along_y(base + n).start()
+            first_along_z(base + n).start()
+
+    def layer(index, origin):
         cut = lax.rem(index, cuts)
         start = pl.multiple_of(cut * ROWS, ROWS)
         rows = pl.ds(start, ROWS)
-
-        input_copy(index).wait()
-
-        hidden = arrived[index].astype(jnp.float32)
-        normed = (hidden * inverse_norm(hidden)).astype(bf16)
-        queries = jnp.dot(normed, wq[...], preferred_element_type=jnp.float32)
-        keys = jnp.dot(normed, wk[...], preferred_element_type=jnp.float32)
-        values = jnp.dot(normed, wv[...], preferred_element_type=jnp.float32)
-
-        @pl.when(me == 0)
-        def _():
-            first[index] = values.astype(bf16)
-            first_along_y(index).start()
-
-        @pl.when(jnp.logical_or(me == 1, me >= half))
-        def _():
-            first_along_y(index).wait_recv()
-
-        @pl.when(jnp.logical_and(passes_on, index + lead < pieces))
-        def _():
-            pass_on(index + lead)
-
-        @pl.when(me < half)
-        def _():
-            first_along_z(index).start()
-
-        used = share * values + (1.0 - share) * first[index].astype(jnp.float32)
-        value_cache[rows, :] = used.astype(bf16)
-
-        heads = [slice(n * head_dim, (n + 1) * head_dim) for n in range(HEADS)]
-        for head in heads:
-            part = keys[:, head]
-            key_cache[rows, head] = (part * inverse_norm(part)).astype(bf16)
-        query_parts = []
-        for head in heads:
-            part = queries[:, head]
-            query_parts.append((part * inverse_norm(part)).astype(bf16))
-        query_at = start + lax.broadcasted_iota(jnp.int32, (ROWS, seq), 0)
-        key_at = lax.broadcasted_iota(jnp.int32, (ROWS, seq), 1)
+        packed = arrived[index]
+        hidden = packed.astype(f32)
+        scale = inverse_norm(hidden)
+        query_at = start + lax.broadcasted_iota(jnp.int32, (2 * ROWS, seq), 0) % ROWS
+        key_at = lax.broadcasted_iota(jnp.int32, (2 * ROWS, seq), 1)
         causal = query_at >= key_at
-        probabilities = []
-        for head, part in zip(heads, query_parts):
+        blank = jnp.zeros((ROWS, head_dim), bf16)
+        pair = 2 * head_dim
+        depth = width // 2
+
+        def queries_keys(columns):
+            return [
+                scale * jnp.dot(packed, w[:, columns], preferred_element_type=f32)
+                for w in (wq, wk)
+            ]
+
+        def used_values(columns):
+            if origin:
+                value_cache[rows, columns] = first[index, :, columns]
+                return
+            values = scale * (
+                jnp.dot(
+                    packed[:, :depth], wv[:depth, columns], preferred_element_type=f32
+                )
+                + jnp.dot(
+                    packed[:, depth:], wv[depth:, columns], preferred_element_type=f32
+                )
+            )
+            used = share * values + (1.0 - share) * first[index, :, columns].astype(f32)
+            value_cache[rows, columns] = used.astype(bf16)
+
+        def score(columns, queries, keys):
+            halves = (slice(0, head_dim), slice(head_dim, pair))
+            normed = [
+                [(t[:, h] * inverse_norm(t[:, h])).astype(bf16) for h in halves]
+                for t in (queries, keys)
+            ]
+            key_cache[rows, columns] = jnp.concatenate(normed[1], axis=1)
+            low, high = normed[0]
+            left = jnp.concatenate(
+                [
+                    jnp.concatenate([low, blank], axis=1),
+                    jnp.concatenate([blank, high], axis=1),
+                ],
+                axis=0,
+            )
             scores = score_scale * lax.dot_general(
-                part,
-                key_cache[:, head],
+                left,
+                key_cache[:, columns],
                 (((1,), (1,)), ((), ())),
-                preferred_element_type=jnp.float32,
+                preferred_element_type=f32,
             )
             weights = jnp.where(causal, jnp.exp(scores), 0.0)
-            total = jnp.sum(weights, axis=-1, keepdims=True)
-            probabilities.append((weights * (1.0 / total)).astype(bf16))
-        attended = jnp.concatenate(
-            [
-                jnp.dot(
-                    part, value_cache[:, head], preferred_element_type=jnp.float32
-                ).astype(bf16)
-                for head, part in zip(heads, probabilities)
-            ],
-            axis=1,
-        )
-        added = jnp.dot(attended, wo[...], preferred_element_type=jnp.float32)
-        following = (hidden + added).astype(bf16)
+            return weights.astype(bf16), 1.0 / jnp.sum(weights, axis=-1, keepdims=True)
+
+        def attend(columns, weights, inverse):
+            both = (
+                jnp.dot(weights, value_cache[:, columns], preferred_element_type=f32)
+                * inverse
+            ).astype(bf16)
+            return jnp.concatenate(
+                [both[:ROWS, :head_dim], both[ROWS:, head_dim:]], axis=1
+            )
+
+        def expand(columns, attended):
+            return jnp.dot(attended, wo[columns, :], preferred_element_type=f32)
+
+        c0, c1, c2 = [slice(n * pair, (n + 1) * pair) for n in range(HEADS // 2)]
+        p0 = queries_keys(c0)
+        p1 = queries_keys(c1)
+        p2 = queries_keys(c2)
+        s0 = score(c0, *p0)
+        used_values(c0)
+        s1 = score(c1, *p1)
+        used_values(c1)
+        s2 = score(c2, *p2)
+        used_values(c2)
+        a0 = attend(c0, *s0)
+        a1 = attend(c1, *s1)
+        a2 = attend(c2, *s2)
+        e = expand(slice(0, 3 * pair), jnp.concatenate([a0, a1, a2], axis=1))
+        following = (hidden + e).astype(bf16)
         leaving[index] = following
-
-        @pl.when(me < last)
-        def _():
+        return following
+
+    @pl.when(me == 0)
+    def _():
+        weight_copies[0].wait()
+        make_first(0)
+        for n in range(DIRECT):
+            first_direct(n).start()
+        for copy in weight_copies[1:]:
+            copy.wait()
+
+        @pl.loop(0, pieces)
+        def _(index):
+            layer(index, True)
             hidden_copy(index).start()
 
-        @pl.when(me == last)
-        def _():
-            @pl.when(index // cuts < last)
-            def _():
-                result_copy(index).start()
-
-            @pl.when(index // cuts == last)
-            def _():
-                result[cut] = following
+            @pl.when(jnp.logical_and(index % 2 == 0, index // 2 + 1 < micro))
+            def _():
+                make_first(index // 2 + 1)
+
+    @pl.when(me > 0)
+    def _():
+        for copy in weight_copies:
+            copy.wait()
+
+        @pl.when(passes_on)
+        def _():
+            @pl.loop(0, lead)
+            def _(index):
+                pass_on(index)
+
+        @pl.loop(0, pieces)
+        def _(index):
+            @pl.when(jnp.logical_and(passes_on, index + lead < pieces))
+            def _():
+                pass_on(index + lead)
+
+            hidden_copy(index).wait_recv()
+
+            @pl.when(jnp.logical_or(me == 1, me >= half))
+            def _():
+                first_along_y(index).wait_recv()
+
+            @pl.when(me == 1)
+            def _():
+                first_along_z(index).start()
+
+            @pl.when(me == half)
+            def _():
+                first_along_y(index).start()
+
+            following = layer(index, False)
+
+            @pl.when(me < last)
+            def _():
+                hidden_copy(index).start()
+
+            @pl.when(me == last)
+            def _():
+                @pl.when(index // cuts < last)
+                def _():
+                    result_copy(index).start()
+
+                @pl.when(index // cuts == last)
+                def _():
+                    result[lax.rem(index, cuts)] = following
 
     @pl.when(me < last)
     def _():
@@ -257,13 +353,23 @@
         def _():
             hidden_copy(index).wait_send()
 
-        @pl.when(jnp.logical_or(me == 0, passes_on))
+        @pl.when(
+            jnp.logical_or(
+                jnp.logical_or(me % half == 0, me == half - 1),
+                jnp.logical_and(passes_on, index >= DIRECT),
+            )
+        )
         def _():
             first_along_y(index).wait_send()
 
-        @pl.when(me < half)
+        @pl.when(me < half - 1)
         def _():
             first_along_z(index).wait_send()
+
+    @pl.when(me == 0)
+    def _():
+        for n in range(DIRECT):
+            first_direct(n).wait_send()
 
     for copy in out_copies:
         copy.wait()
@@ -299,6 +405,7 @@
             dma((pieces,)),
             dma((pieces,)),
             dma((pieces,)),
+            dma((DIRECT,)),
             dma((cuts,)),
             dma((cuts,)),
         ],

time: 161 us -> 125 us (0.78); the launches traced: 161 us -> 123 us
  Pallas kernels: 159 us -> 121 us
    pallas_call x1, Pallas kernels: 159 us -> 121 us  [body(): pl.pallas_call(functools.partial(kernel, sections), out_shape=jax.ShapeDt...]
where the time goes in v2:
time: 125 us; the launch traced here: 123 us
  Pallas kernels  121 us (97%)
  local copies, waits for them, and re-layouts  1.77 us (1%)
    pallas_call x1, Pallas kernels, body(): pl.pallas_call(functools.partial(kernel, sections), out_shape=jax.ShapeDt...  121 us

profile of v2, /device:TPU:184, one launch (start us, length us, event | category | flops | bytes accessed | tf_op | source)
XLA Modules:
  0.0 123.3 jit_solution(7252951469089233984)
XLA Ops:
  0.7 120.9 %shard_map.64 = bf16[1,128,1536]{2,1,0:T(8,128)(2,1)} custom-call(bf16[8,128,1536]{2,1,0:T(8,128)(2,1)} %x_hbm.1, bf16[1,1536,768]{2,1,0:T(8,128)(2,1)} %wq_hbm.1, bf16[1,1536,768]{2,1,0:T(8,128)(2,1)} %wk_hbm.1, bf16[1,1536,768]{2,1,0:T(8,128)(2,1)} %wv_hbm.1, bf16[1,768,1536]{2,1,0:T(8,128)(2,1)} %wo_hbm.1, f32[1]{0:T(128)S(6)} %copy.8.mix_ref), custom_call_target="tpu_custom_call" | custom-call | tf_op jit(solution)/shard_map/pallas_call | solution.py:386
  121.6 1.8 %copy.9 = bf16[1,128,1536]{2,1,0:T(8,128)(2,1)} copy(bf16[1,128,1536]{2,1,0:T(8,128)(2,1)} %shard_map.64) | data formatting | bytes 786432

commit v3 on v2

--- a/solution.py
+++ b/solution.py
@@ -10,7 +10,7 @@
 MESH = pl.DeviceIdType.MESH
 HEADS = 6
 ROWS = 32
-LEAD = {3: 14, 2: 5}
+LEAD = {3: 15, 2: 7}
 DIRECT = 2
 
 epsilon = 1e-06
@@ -29,7 +29,7 @@
     wv_hbm,
     wo_hbm,
     mix_ref,
-    out_hbm,
+    out_ref,
     wq,
     wk,
     wv,
@@ -48,7 +48,6 @@
     first_z_sem,
     first_direct_sem,
     result_sem,
-    out_sem,
 ):
     me = lax.axis_index("section")
     last = sections - 1
@@ -147,8 +146,6 @@
         )
     key_cache[...] = jnp.zeros_like(key_cache)
     value_cache[...] = jnp.zeros_like(value_cache)
-    pl.semaphore_wait(barrier, sections - 1)
-
     f32 = jnp.float32
     passes_on = jnp.logical_and(me >= 2, me < half)
     lead = jnp.where(me == half - 1, LEAD[3], LEAD[2])
@@ -174,9 +171,11 @@
         values = scale * jnp.dot(packed, wv[...], preferred_element_type=f32)
         for n in range(cuts):
             first[base + n] = values[n * ROWS : (n + 1) * ROWS].astype(bf16)
+
+    def send_first(sequence):
         for n in range(cuts):
-            first_along_y(base + n).start()
-            first_along_z(base + n).start()
+            first_along_y(sequence * cuts + n).start()
+            first_along_z(sequence * cuts + n).start()
 
     def layer(index, origin):
         cut = lax.rem(index, cuts)
@@ -190,8 +189,6 @@
         causal = query_at >= key_at
         blank = jnp.zeros((ROWS, head_dim), bf16)
         pair = 2 * head_dim
-        depth = width // 2
-
         def queries_keys(columns):
             return [
                 scale * jnp.dot(packed, w[:, columns], preferred_element_type=f32)
@@ -202,14 +199,7 @@
             if origin:
                 value_cache[rows, columns] = first[index, :, columns]
                 return
-            values = scale * (
-                jnp.dot(
-                    packed[:, :depth], wv[:depth, columns], preferred_element_type=f32
-                )
-                + jnp.dot(
-                    packed[:, depth:], wv[depth:, columns], preferred_element_type=f32
-                )
-            )
+            values = scale * jnp.dot(packed, wv[:, columns], preferred_element_type=f32)
             used = share * values + (1.0 - share) * first[index, :, columns].astype(f32)
             value_cache[rows, columns] = used.astype(bf16)
 
@@ -253,12 +243,10 @@
         p0 = queries_keys(c0)
         p1 = queries_keys(c1)
         p2 = queries_keys(c2)
+        used_values(slice(0, 3 * pair))
         s0 = score(c0, *p0)
-        used_values(c0)
         s1 = score(c1, *p1)
-        used_values(c1)
         s2 = score(c2, *p2)
-        used_values(c2)
         a0 = attend(c0, *s0)
         a1 = attend(c1, *s1)
         a2 = attend(c2, *s2)
@@ -271,6 +259,12 @@
     def _():
         weight_copies[0].wait()
         make_first(0)
+
+    pl.semaphore_wait(barrier, sections - 1)
+
+    @pl.when(me == 0)
+    def _():
+        send_first(0)
         for n in range(DIRECT):
             first_direct(n).start()
         for copy in weight_copies[1:]:
@@ -284,6 +278,7 @@
             @pl.when(jnp.logical_and(index % 2 == 0, index // 2 + 1 < micro))
             def _():
                 make_first(index // 2 + 1)
+                send_first(index // 2 + 1)
 
     @pl.when(me > 0)
     def _():
@@ -338,14 +333,8 @@
         def _(index):
             result_copy(index).wait_recv()
 
-    out_copies = [
-        pltpu.make_async_copy(
-            result.at[n], out_hbm.at[0, pl.ds(n * ROWS, ROWS)], out_sem.at[n]
-        )
-        for n in range(cuts)
-    ]
-    for copy in out_copies:
-        copy.start()
+    for n in range(cuts):
+        out_ref[0, n * ROWS : (n + 1) * ROWS] = result[n]
 
     @pl.loop(0, pieces)
     def _(index):
@@ -370,9 +359,6 @@
     def _():
         for n in range(DIRECT):
             first_direct(n).wait_send()
-
-    for copy in out_copies:
-        copy.wait()
 
 
 def body(inputs, w_query, w_key, w_value, w_out, mixing):
@@ -387,7 +373,7 @@
         functools.partial(kernel, sections),
         out_shape=jax.ShapeDtypeStruct((micro // sections, seq, width), jnp.bfloat16),
         in_specs=[anywhere] * 5 + [pl.BlockSpec(memory_space=pltpu.SMEM)],
-        out_specs=anywhere,
+        out_specs=pl.BlockSpec(memory_space=pltpu.VMEM),
         scratch_shapes=[
             pltpu.VMEM((width, inner), jnp.bfloat16),
             pltpu.VMEM((width, inner), jnp.bfloat16),
@@ -407,10 +393,9 @@
             dma((pieces,)),
             dma((DIRECT,)),
             dma((cuts,)),
-            dma((cuts,)),
         ],
         compiler_params=pltpu.CompilerParams(
-            collective_id=0, has_side_effects=True, vmem_limit_bytes=60 * 2**20
+            collective_id=0, has_side_effects=True, vmem_limit_bytes=53 * 2**20
         ),
     )(inputs, w_query, w_key, w_value, w_out, mixing)
 

time: 125 us -> 121 us (0.968)
  Pallas kernels: 121 us -> 119 us
    pallas_call x1, Pallas kernels: 121 us -> 119 us  [body(): pl.pallas_call(functools.partial(kernel, sections), out_shape=jax.ShapeDt...]
where the time goes in v3:
time: 121 us; the launch traced here: 120 us
  Pallas kernels  119 us (98%)
    pallas_call x1, Pallas kernels, body(): pl.pallas_call(functools.partial(kernel, sections), out_shape=jax.ShapeDt...  119 us

profile of v3, /device:TPU:184, one launch (start us, length us, event | category | flops | bytes accessed | tf_op | source)
XLA Modules:
  0.0 120.5 jit_solution(2973014229549678896)
XLA Ops:
  0.7 119.1 %shard_map.64 = bf16[1,128,1536]{2,1,0:T(8,128)(2,1)S(1)} custom-call(bf16[8,128,1536]{2,1,0:T(8,128)(2,1)} %x_hbm.1, bf16[1,1536,768]{2,1,0:T(8,128)(2,1)} %wq_hbm.1, bf16[1,1536,768]{2,1,0:T(8,128)(2,1)} %wk_hbm.1, bf16[1,1536,768]{2,1,0:T(8,128)(2,1)} %wv_hbm.1, bf16[1,768,1536]{2,1,0:T(8,128)(2,1)} %wo_hbm.1, f32[1]{0:T(128)S(6)} %copy.8.mix_ref), custom_call_target="tpu_custom_call" | custom-call | tf_op jit(solution)/shard_map/pallas_call | solution.py:372
  119.7 0.7 copy.9

commit v4 on v3

--- a/solution.py
+++ b/solution.py
@@ -319,6 +319,10 @@
 
             @pl.when(me == last)
             def _():
+                @pl.when(index >= cuts)
+                def _():
+                    result_copy(index - cuts).wait_send()
+
                 @pl.when(index // cuts < last)
                 def _():
                     result_copy(index).start()
@@ -336,24 +340,24 @@
     for n in range(cuts):
         out_ref[0, n * ROWS : (n + 1) * ROWS] = result[n]
 
-    @pl.loop(0, pieces)
-    def _(index):
-        @pl.when(jnp.logical_or(me < last, index // cuts < last))
-        def _():
+    @pl.when(me < last)
+    def _():
+        @pl.loop(0, pieces)
+        def _(index):
             hidden_copy(index).wait_send()
 
-        @pl.when(
-            jnp.logical_or(
-                jnp.logical_or(me % half == 0, me == half - 1),
-                jnp.logical_and(passes_on, index >= DIRECT),
+            @pl.when(
+                jnp.logical_or(
+                    jnp.logical_or(me % half == 0, me == half - 1),
+                    jnp.logical_and(passes_on, index >= DIRECT),
+                )
             )
-        )
-        def _():
-            first_along_y(index).wait_send()
-
-        @pl.when(me < half - 1)
-        def _():
-            first_along_z(index).wait_send()
+            def _():
+                first_along_y(index).wait_send()
+
+            @pl.when(me < half - 1)
+            def _():
+                first_along_z(index).wait_send()
 
     @pl.when(me == 0)
     def _():

time: 121 us -> 120 us (level)
  no operation moved by 1% of the time
where the time goes in v4:
time: 120 us
  Pallas kernels  118 us (98%)
    pallas_call x1, Pallas kernels, body(): pl.pallas_call(functools.partial(kernel, sections), out_shape=jax.ShapeDt...  118 us

profile of v4, /device:TPU:184, one launch (start us, length us, event | category | flops | bytes accessed | tf_op | source)
XLA Modules:
  0.0 119.9 jit_solution(17489729140062720329)
XLA Ops:
  0.7 118.5 %shard_map.64 = bf16[1,128,1536]{2,1,0:T(8,128)(2,1)S(1)} custom-call(bf16[8,128,1536]{2,1,0:T(8,128)(2,1)} %x_hbm.1, bf16[1,1536,768]{2,1,0:T(8,128)(2,1)} %wq_hbm.1, bf16[1,1536,768]{2,1,0:T(8,128)(2,1)} %wk_hbm.1, bf16[1,1536,768]{2,1,0:T(8,128)(2,1)} %wv_hbm.1, bf16[1,768,1536]{2,1,0:T(8,128)(2,1)} %wo_hbm.1, f32[1]{0:T(128)S(6)} %copy.8.mix_ref), custom_call_target="tpu_custom_call" | custom-call | tf_op jit(solution)/shard_map/pallas_call | solution.py:376
  119.1 0.7 copy.9
